TPU v7x, 32 devices: a whole 2x2x4 slice. The times are simulated.
32 devices in a mesh: head: 2 (over x), inner: 4 (over y, core), outer: 4 (over z).
Axes of the slice: x: 2, y: 2, z: 4, core: 2. Of those that a mesh axis runs over, the one named last changes fastest.
Arguments:
- queries: float32 [2048, 8, 128], P(('inner', 'outer'), 'head'), may hold values from -8 to 8
- key_rows: float32 [2048, 128], P(('inner', 'outer'), 'head'), may hold values from -8 to 8
- values: float32 [2048, 128], P(('inner', 'outer'), 'head'), may hold values from -24 to 24
- out_grad: float32 [2048, 8, 128], P(('inner', 'outer'), 'head'), may hold values from -48 to 48
- sink_len: int32 [1], replicated, may hold values from 32 to 128
- window_len: int32 [1], replicated, may hold values from 129 to 640
- block_codes: int32 [16, 5], replicated, may hold values from 0 to 2, as said below
Outputs:
- query_grad: float32 [2048, 8, 128], P(('inner', 'outer'), 'head')
- key_grad: float32 [2048, 128], P(('inner', 'outer'), 'head')
- value_grad: float32 [2048, 128], P(('inner', 'outer'), 'head')
Inputs may be any that keep to these rules, and one draw needn't show every extreme that they name: block_codes[b, 0] is 1 or 2 for every block b.
All inputs are finite; a program needn't handle non-finite values.
Results may differ from a plain program's by a relative error of at most 0.0003.
Values sent between devices are 32-bit elements; how exact they have to be, the bound alone decides.
A program may use at most 64 MiB of HBM per device.

v0:
```python
import math
import jax
import jax.numpy as jnp
from jax import lax
from jax.sharding import PartitionSpec as P

STEPS = 5
SINK = 128
very_low = -1e30
precise = lax.Precision.HIGHEST


def swapped(array, axis, distance):
    return lax.ppermute(array, axis, [(i, i ^ 1 << distance) for i in range(lax.axis_size(axis))])


def spread(array, axis, root):
    mine = lax.axis_index(axis) == root
    return lax.psum(jnp.where(mine, array, jnp.zeros_like(array)), axis)


def shifted(value, axis, steps):
    count = lax.axis_size(axis)
    pairs = [(source, (source + steps) % count) for source in range(count)]
    return lax.ppermute(value, axis, pairs)


def codes_for(block_codes, query_block, offset):
    row_ids = jnp.arange(block_codes.shape[0], dtype=jnp.int32)
    return jnp.sum(jnp.where(row_ids == query_block, block_codes[:, offset], 0))


def visible(query_block, key_block, offset, block_rows, sink_end, window, block_codes, present):
    local_ids = jnp.arange(block_rows, dtype=jnp.int32)
    pos_q = query_block * block_rows + local_ids
    pos_k = key_block * block_rows + local_ids
    code = codes_for(block_codes, query_block, offset)
    near = pos_q[:, None] - pos_k[None, :] < window
    rule = (code != 0) & ((code == 2) | near)
    in_sink = (pos_k < sink_end)[None, :]
    chosen = jnp.where(query_block == 0, in_sink | rule, jnp.logical_not(in_sink) & rule)
    return present & (pos_k[None, :] <= pos_q[:, None]) & chosen


def scores(query_blk, key_blk, temper):
    return temper * jnp.einsum("qhd,kd->hqk", query_blk, key_blk, precision=precise)


def forward_step(running, query_blk, key_blk, value_blk, allowed, temper):
    row_max, row_sum, carried = running
    logits = jnp.where(allowed[None], scores(query_blk, key_blk, temper), very_low)
    new_max = jnp.maximum(row_max, jnp.max(logits, axis=2))
    factor = jnp.exp(row_max - new_max)
    weights = jnp.where(allowed[None], jnp.exp(logits - new_max[:, :, None]), 0.0)
    row_sum = row_sum * factor + jnp.sum(weights, axis=2)
    carried = carried * factor[:, :, None] + jnp.einsum(
        "hqk,kd->hqd", weights, value_blk, precision=precise
    )
    return ((new_max, row_sum, carried), logits)


def finish(running, grad_blk):
    row_max, row_sum, carried = running
    log_sum = row_max + jnp.log(row_sum)
    row_delta = jnp.sum(jnp.transpose(grad_blk, (1, 0, 2)) * carried, axis=2) / row_sum
    return (log_sum, row_delta)


def backward_step(
    query_blk, grad_blk, log_sum, row_delta, key_blk, value_blk, allowed, temper, cached
):
    if cached is None:
        cached = scores(query_blk, key_blk, temper)
    weights = jnp.where(allowed[None], jnp.exp(cached - log_sum[:, :, None]), 0.0)
    grad_dots = jnp.einsum("qhd,kd->hqk", grad_blk, value_blk, precision=precise)
    dscores = weights * (grad_dots - row_delta[:, :, None])
    step_dq = temper * jnp.einsum("hqk,kd->qhd", dscores, key_blk, precision=precise)
    step_dk = temper * jnp.einsum("hqk,qhd->kd", dscores, query_blk, precision=precise)
    step_dv = jnp.einsum("hqk,qhd->kd", weights, grad_blk, precision=precise)
    return (step_dq, step_dk, step_dv)


def shards(queries, key_rows, values, out_grad, sink_len, window_len, block_codes):
    block_rows, heads_dev, head_dim = queries.shape
    temper = 1.0 / math.sqrt(head_dim)
    sink_end = sink_len[0]
    window = window_len[0]
    seq_index = lax.axis_index(("inner", "outer"))
    seq_count = lax.axis_size(("inner", "outer"))
    upper_half = lax.axis_index("head") % 2 == 1
    other_keys, other_values = swapped((key_rows, values), "head", 0)
    key_full = jnp.where(
        upper_half,
        jnp.concatenate([other_keys, key_rows], 1),
        jnp.concatenate([key_rows, other_keys], 1),
    )
    value_full = jnp.where(
        upper_half,
        jnp.concatenate([other_values, values], 1),
        jnp.concatenate([values, other_values], 1),
    )
    sink_keys, sink_values = (
        spread(key_full, ("inner", "outer"), 0),
        spread(value_full, ("inner", "outer"), 0),
    )
    sink_ids = jnp.arange(SINK, dtype=jnp.int32)
    sink_allowed = jnp.broadcast_to(
        ((seq_index >= 1) & (sink_ids < sink_end))[None, :], (block_rows, SINK)
    )
    carried = jnp.zeros((heads_dev, block_rows, head_dim), jnp.float32)
    running = (
        jnp.full((heads_dev, block_rows), very_low, jnp.float32),
        jnp.zeros((heads_dev, block_rows), jnp.float32),
        carried,
    )
    running, ignored = forward_step(running, queries, sink_keys, sink_values, sink_allowed, temper)
    grad_keys = jnp.zeros((block_rows, head_dim), jnp.float32)
    grad_values = jnp.zeros((block_rows, head_dim), jnp.float32)
    moving_k, moving_v = (key_full, value_full)
    cached = None
    for offset in range(STEPS):
        if offset > 0:
            moving_k, moving_v = shifted((moving_k, moving_v), ("inner", "outer"), 1)
        allowed = visible(
            seq_index,
            (seq_index - offset) % seq_count,
            offset,
            block_rows,
            sink_end,
            window,
            block_codes,
            seq_index - offset >= 0,
        )
        running, cached = forward_step(running, queries, moving_k, moving_v, allowed, temper)
    log_sum, row_delta = finish(running, out_grad)
    grad_q = jnp.zeros_like(queries)
    for offset in range(STEPS - 1, -1, -1):
        if offset < STEPS - 1:
            moving_k, moving_v, grad_keys, grad_values = shifted(
                (moving_k, moving_v, grad_keys, grad_values), ("inner", "outer"), -1
            )
            cached = None
        allowed = visible(
            seq_index,
            (seq_index - offset) % seq_count,
            offset,
            block_rows,
            sink_end,
            window,
            block_codes,
            seq_index - offset >= 0,
        )
        step_dq, step_dk, step_dv = backward_step(
            queries, out_grad, log_sum, row_delta, moving_k, moving_v, allowed, temper, cached
        )
        grad_q = grad_q + step_dq
        grad_keys = grad_keys + step_dk
        grad_values = grad_values + step_dv
    sink_dq, sink_dk, sink_dv = backward_step(
        queries, out_grad, log_sum, row_delta, sink_keys, sink_values, sink_allowed, temper, None
    )
    grad_q = grad_q + sink_dq
    total_dk, total_dv = lax.psum((sink_dk, sink_dv), ("inner", "outer"))
    is_first = seq_index == 0
    grad_keys = grad_keys.at[:SINK].add(jnp.where(is_first, total_dk, 0.0))
    grad_values = grad_values.at[:SINK].add(jnp.where(is_first, total_dv, 0.0))
    half_cols = key_rows.shape[1]
    keep_k = jnp.where(upper_half, grad_keys[:, half_cols:], grad_keys[:, :half_cols])
    send_k = jnp.where(upper_half, grad_keys[:, :half_cols], grad_keys[:, half_cols:])
    keep_v = jnp.where(upper_half, grad_values[:, half_cols:], grad_values[:, :half_cols])
    send_v = jnp.where(upper_half, grad_values[:, :half_cols], grad_values[:, half_cols:])
    got_k, got_v = swapped((send_k, send_v), "head", 0)
    return (grad_q, keep_k + got_k, keep_v + got_v)


def solution(mesh):
    in_specs = (
        P(("inner", "outer"), "head", None),
        P(("inner", "outer"), "head"),
        P(("inner", "outer"), "head"),
        P(("inner", "outer"), "head", None),
        P(),
        P(),
        P(),
    )
    out_specs = (
        P(("inner", "outer"), "head", None),
        P(("inner", "outer"), "head"),
        P(("inner", "outer"), "head"),
    )
    return jax.shard_map(shards, mesh=mesh, in_specs=in_specs, out_specs=out_specs, check_vma=False)
```

profile of v0, /device:TPU:8, one launch (start us, length us, event | category | flops | bytes accessed | tf_op | source)
XLA Modules:
  0.0 250.2 jit_solution(6072486249846511252)
XLA Ops:
  7.2 0.9 copy.10
  8.1 1.6 collective-permute-start
  9.8 0.6 collective-permute-start.5
  10.4 0.7 copy-done.6
  11.1 0.7 fusion.159
  20.8 0.7 broadcast_select_fusion.1
  21.6 1.6 collective-permute-start.1
  23.2 0.7 broadcast_select_fusion
  23.9 1.6 collective-permute-start.6
  26.2 1.6 collective-permute-start.2
  28.2 88.4 %all-reduce.7.cloned.1.call-done = (f32[128,128]{1,0:T(8,128)}, f32[128,128]{1,0:T(8,128)}) async-done(((f32[128,128]{1,0:T(8,128)}, f32[128,128]{1,0:T(8,128)}), (f32[128,128]{1,0:T(8,128)}, f32[128,128]{1,0:T(8,128)})) %all-reduce.7.cloned.1.call-update) | async-done | bytes 131088 | tf_op jit(solution)/shard_map/psum | solution.py:19
  116.6 1.2 select_reduce_fusion
  117.9 2.0 collective-permute-start.3
  120.3 1.8 collective-permute-done.7
  122.2 0.7 collective-permute-done.3
  122.9 1.3 collective-permute-start.4
  124.6 1.8 collective-permute-done.8
  126.4 0.7 collective-permute-start.9
  127.2 1.4 collective-permute-done.4
  129.5 0.4 convolution_bitcast_fusion.11
  130.4 0.5 fusion.20
  131.3 0.4 fusion.18
  131.8 0.4 fusion.17
  132.2 0.4 fusion.16
  132.7 1.1 convolution_bitcast_fusion.6
  133.7 0.4 fusion.48
  134.6 1.0 fusion.49
  136.0 4.2 %collective-permute-start.23 = (f32[128,128]{1,0:T(8,128)S(1)}, f32[128,128]{1,0:T(8,128)S(1)}, u32[]{:S(2)}, u32[]{:S(2)}) collective-permute-start(f32[128,128]{1,0:T(8,128)S(1)} %convolution_bitcast_fusion.11), channel_id=1, source_target_pairs={{0,15},{1,0},{2,1},{3,2},{4,3},{5,4},{6,5},{7,6},{8,7},{9,8},{10,9... | collective-permute-start | bytes 196616 | tf_op jit(solution)/shard_map/ppermute | solution.py:25
  141.0 1.1 collective-permute-start.18
  142.7 3.8 %collective-permute-done.10 = f32[128,128]{1,0:T(8,128)S(1)} collective-permute-done((f32[128,128]{1,0:T(8,128)S(1)}, f32[128,128]{1,0:T(8,128)S(1)}, u32[]{:S(2)}, u32[]{:S(2)}) %collective-permute-start.10) | collective-permute-done | bytes 65568 | tf_op jit(solution)/shard_map/ppermute | solution.py:25
  147.3 1.3 collective-permute-start.24
  149.4 2.3 collective-permute-start.19
  152.3 4.2 %collective-permute-done.12 = f32[128,128]{1,0:T(8,128)S(1)} collective-permute-done((f32[128,128]{1,0:T(8,128)S(1)}, f32[128,128]{1,0:T(8,128)S(1)}, u32[]{:S(2)}, u32[]{:S(2)}) %collective-permute-start.12) | collective-permute-done | bytes 65568 | tf_op jit(solution)/shard_map/ppermute | solution.py:25
  157.3 1.8 collective-permute-start.25
  159.9 1.9 collective-permute-start.20
  161.9 0.5 collective-permute-start.14
  162.9 3.8 %collective-permute-done.14 = f32[128,128]{1,0:T(8,128)S(1)} collective-permute-done((f32[128,128]{1,0:T(8,128)S(1)}, f32[128,128]{1,0:T(8,128)S(1)}, u32[]{:S(2)}, u32[]{:S(2)}) %collective-permute-start.14) | collective-permute-done | bytes 65568 | tf_op jit(solution)/shard_map/ppermute | solution.py:25
  167.6 1.7 collective-permute-start.26
  170.1 2.8 %collective-permute-start.21 = (f32[128,128]{1,0:T(8,128)S(1)}, f32[128,128]{1,0:T(8,128)S(1)}, u32[]{:S(2)}, u32[]{:S(2)}) collective-permute-start(f32[128,128]{1,0:T(8,128)S(1)} %add.352), channel_id=1, source_target_pairs={{0,15},{1,0},{2,1},{3,2},{4,3},{5,4},{6,5},{7,6},{8,7},{9,8},{10,9... | collective-permute-start | bytes 196616 | tf_op jit(solution)/shard_map/ppermute | solution.py:25
  173.6 3.6 %collective-permute-done.16 = f32[128,128]{1,0:T(8,128)S(1)} collective-permute-done((f32[128,128]{1,0:T(8,128)S(1)}, f32[128,128]{1,0:T(8,128)S(1)}, u32[]{:S(2)}, u32[]{:S(2)}) %collective-permute-start.16) | collective-permute-done | bytes 65568 | tf_op jit(solution)/shard_map/ppermute | solution.py:25
  177.9 57.4 %all-reduce.5.cloned.1.call-done = (f32[128,128]{1,0:T(8,128)}, f32[128,128]{1,0:T(8,128)}) async-done(((f32[128,128]{1,0:T(8,128)}, f32[128,128]{1,0:T(8,128)}), (f32[128,128]{1,0:T(8,128)}, f32[128,128]{1,0:T(8,128)})) %all-reduce.5.cloned.1.call-update) | async-done | bytes 131088 | tf_op jit(solution)/shard_map/psum | solution.py:163
  235.4 1.5 collective-permute-start.27
  238.3 0.6 collective-permute-start.22
  238.9 0.4 fusion.2
  239.4 0.8 copy.78
  240.3 0.7 copy.80
  241.0 1.6 collective-permute-done.22
  242.7 0.7 copy.79
  (112 shorter events, 16.2 us)
Async XLA Ops:
  7.2 18.3 %copy-start = (f32[128,4,128]{2,1,0:T(4,128)S(1)}, f32[128,4,128]{2,1,0:T(4,128)}, u32[]{:S(2)}) copy-start(f32[128,4,128]{2,1,0:T(4,128)} %param.15) | copy-start | bytes 786436
  7.2 2.5 copy-start.5
  7.2 109.4 %all-reduce.7.cloned.1.call-start = ((), (), s32[]{:S(2)}) async-start(), calls=%async_computation.1 | async-start | bytes 262144 | tf_op jit(solution)/shard_map/psum | solution.py:19
  8.1 12.7 %collective-permute-start = (f32[128,64]{1,0:T(8,128)S(1)}, f32[128,64]{1,0:T(8,128)S(1)}, u32[]{:S(2)}, u32[]{:S(2)}) collective-permute-start(f32[128,64]{1,0:T(8,128)S(1)} %copy.10), channel_id=1, source_target_pairs={{0,16},{16,0},{1,17},{17,1},{2,18},{18,2},{3,19},{19,3},{4,20},{20... | collective-permute-start | bytes 98312 | tf_op jit(solution)/shard_map/ppermute | solution.py:14
  9.8 13.4 %collective-permute-start.5 = (f32[128,64]{1,0:T(8,128)S(1)}, f32[128,64]{1,0:T(8,128)S(1)}, u32[]{:S(2)}, u32[]{:S(2)}) collective-permute-start(f32[128,64]{1,0:T(8,128)S(1)} %copy.24), channel_id=1, source_target_pairs={{0,16},{16,0},{1,17},{17,1},{2,18},{18,2},{3,19},{19,3},{4,20},{20... | collective-permute-start | bytes 98312 | tf_op jit(solution)/shard_map/ppermute | solution.py:14
  10.4 0.7 copy-start.6
  10.4 10.3 %copy-start.1 = (f32[128,4,128]{2,1,0:T(4,128)S(1)}, f32[128,4,128]{2,1,0:T(4,128)}, u32[]{:S(2)}) copy-start(f32[128,4,128]{2,1,0:T(4,128)} %param.18) | copy-start | bytes 786436
  21.6 4.6 %collective-permute-start.1 = (f32[128,128]{1,0:T(8,128)S(1)}, f32[128,128]{1,0:T(8,128)S(1)}, u32[]{:S(2)}, u32[]{:S(2)}) collective-permute-start(f32[128,128]{1,0:T(8,128)S(1)} %get-tuple-element.80), channel_id=1, source_target_pairs={{0,1},{1,2},{2,3},{3,4},{4,5},{5,6},{6,7},{7,8},{8,9},{9,10},{10,1... | collective-permute-start | bytes 196616 | tf_op jit(solution)/shard_map/ppermute | solution.py:25
  23.9 94.0 %collective-permute-start.6 = (f32[128,128]{1,0:T(8,128)S(1)}, f32[128,128]{1,0:T(8,128)S(1)}, u32[]{:S(2)}, u32[]{:S(2)}) collective-permute-start(f32[128,128]{1,0:T(8,128)S(1)} %get-tuple-element.78), channel_id=1, source_target_pairs={{0,1},{1,2},{2,3},{3,4},{4,5},{5,6},{6,7},{7,8},{8,9},{9,10},{10,1... | collective-permute-start | bytes 196616 | tf_op jit(solution)/shard_map/ppermute | solution.py:25
  25.9 209.4 %all-reduce.5.cloned.1.call-start = ((), (), s32[]{:S(2)}) async-start(), calls=%async_computation | async-start | bytes 262144 | tf_op jit(solution)/shard_map/psum | solution.py:163
  26.2 91.7 %collective-permute-start.2 = (f32[128,128]{1,0:T(8,128)S(1)}, f32[128,128]{1,0:T(8,128)S(1)}, u32[]{:S(2)}, u32[]{:S(2)}) collective-permute-start(f32[128,128]{1,0:T(8,128)S(1)} %collective-permute-done.1), channel_id=1, source_target_pairs={{0,1},{1,2},{2,3},{3,4},{4,5},{5,6},{6,7},{7,8},{8,9},{9,10},{10,1... | collective-permute-start | bytes 196616 | tf_op jit(solution)/shard_map/ppermute | solution.py:25
  117.8 4.3 %collective-permute-start.7 = (f32[128,128]{1,0:T(8,128)S(1)}, f32[128,128]{1,0:T(8,128)S(1)}, u32[]{:S(2)}, u32[]{:S(2)}) collective-permute-start(f32[128,128]{1,0:T(8,128)S(1)} %collective-permute-done.6), channel_id=1, source_target_pairs={{0,1},{1,2},{2,3},{3,4},{4,5},{5,6},{6,7},{7,8},{8,9},{9,10},{10,1... | collective-permute-start | bytes 196616 | tf_op jit(solution)/shard_map/ppermute | solution.py:25
  117.9 4.9 %collective-permute-start.3 = (f32[128,128]{1,0:T(8,128)S(1)}, f32[128,128]{1,0:T(8,128)S(1)}, u32[]{:S(2)}, u32[]{:S(2)}) collective-permute-start(f32[128,128]{1,0:T(8,128)S(1)} %collective-permute-done.2), channel_id=1, source_target_pairs={{0,1},{1,2},{2,3},{3,4},{4,5},{5,6},{6,7},{7,8},{8,9},{9,10},{10,1... | collective-permute-start | bytes 196616 | tf_op jit(solution)/shard_map/ppermute | solution.py:25
  122.2 4.3 %collective-permute-start.8 = (f32[128,128]{1,0:T(8,128)S(1)}, f32[128,128]{1,0:T(8,128)S(1)}, u32[]{:S(2)}, u32[]{:S(2)}) collective-permute-start(f32[128,128]{1,0:T(8,128)S(1)} %collective-permute-done.7), channel_id=1, source_target_pairs={{0,1},{1,2},{2,3},{3,4},{4,5},{5,6},{6,7},{7,8},{8,9},{9,10},{10,1... | collective-permute-start | bytes 196616 | tf_op jit(solution)/shard_map/ppermute | solution.py:25
  122.9 5.7 %collective-permute-start.4 = (f32[128,128]{1,0:T(8,128)S(1)}, f32[128,128]{1,0:T(8,128)S(1)}, u32[]{:S(2)}, u32[]{:S(2)}) collective-permute-start(f32[128,128]{1,0:T(8,128)S(1)} %collective-permute-done.3), channel_id=1, source_target_pairs={{0,1},{1,2},{2,3},{3,4},{4,5},{5,6},{6,7},{7,8},{8,9},{9,10},{10,1... | collective-permute-start | bytes 196616 | tf_op jit(solution)/shard_map/ppermute | solution.py:25
  126.4 7.3 %collective-permute-start.9 = (f32[128,128]{1,0:T(8,128)S(1)}, f32[128,128]{1,0:T(8,128)S(1)}, u32[]{:S(2)}, u32[]{:S(2)}) collective-permute-start(f32[128,128]{1,0:T(8,128)S(1)} %collective-permute-done.8), channel_id=1, source_target_pairs={{0,1},{1,2},{2,3},{3,4},{4,5},{5,6},{6,7},{7,8},{8,9},{9,10},{10,1... | collective-permute-start | bytes 196616 | tf_op jit(solution)/shard_map/ppermute | solution.py:25
  129.5 0.8 copy-start.3
  134.6 1.0 copy-start.2
  136.0 10.9 %collective-permute-start.23 = (f32[128,128]{1,0:T(8,128)S(1)}, f32[128,128]{1,0:T(8,128)S(1)}, u32[]{:S(2)}, u32[]{:S(2)}) collective-permute-start(f32[128,128]{1,0:T(8,128)S(1)} %convolution_bitcast_fusion.11), channel_id=1, source_target_pairs={{0,15},{1,0},{2,1},{3,2},{4,3},{5,4},{6,5},{7,6},{8,7},{9,8},{10,9... | collective-permute-start | bytes 196616 | tf_op jit(solution)/shard_map/ppermute | solution.py:25
  141.0 8.0 %collective-permute-start.18 = (f32[128,128]{1,0:T(8,128)S(1)}, f32[128,128]{1,0:T(8,128)S(1)}, u32[]{:S(2)}, u32[]{:S(2)}) collective-permute-start(f32[128,128]{1,0:T(8,128)S(1)} %fusion.54), channel_id=1, source_target_pairs={{0,15},{1,0},{2,1},{3,2},{4,3},{5,4},{6,5},{7,6},{8,7},{9,8},{10,9... | collective-permute-start | bytes 196616 | tf_op jit(solution)/shard_map/ppermute | solution.py:25
  142.2 4.3 %collective-permute-start.10 = (f32[128,128]{1,0:T(8,128)S(1)}, f32[128,128]{1,0:T(8,128)S(1)}, u32[]{:S(2)}, u32[]{:S(2)}) collective-permute-start(f32[128,128]{1,0:T(8,128)S(1)} %collective-permute-done.4), channel_id=1, source_target_pairs={{0,15},{1,0},{2,1},{3,2},{4,3},{5,4},{6,5},{7,6},{8,7},{9,8},{10,9... | collective-permute-start | bytes 196616 | tf_op jit(solution)/shard_map/ppermute | solution.py:25
  142.2 6.4 %collective-permute-start.11 = (f32[128,128]{1,0:T(8,128)S(1)}, f32[128,128]{1,0:T(8,128)S(1)}, u32[]{:S(2)}, u32[]{:S(2)}) collective-permute-start(f32[128,128]{1,0:T(8,128)S(1)} %collective-permute-done.9), channel_id=1, source_target_pairs={{0,15},{1,0},{2,1},{3,2},{4,3},{5,4},{6,5},{7,6},{8,7},{9,8},{10,9... | collective-permute-start | bytes 196616 | tf_op jit(solution)/shard_map/ppermute | solution.py:25
  147.3 10.0 %collective-permute-start.24 = (f32[128,128]{1,0:T(8,128)S(1)}, f32[128,128]{1,0:T(8,128)S(1)}, u32[]{:S(2)}, u32[]{:S(2)}) collective-permute-start(f32[128,128]{1,0:T(8,128)S(1)} %fusion.56), channel_id=1, source_target_pairs={{0,15},{1,0},{2,1},{3,2},{4,3},{5,4},{6,5},{7,6},{8,7},{9,8},{10,9... | collective-permute-start | bytes 196616 | tf_op jit(solution)/shard_map/ppermute | solution.py:25
  149.4 10.5 %collective-permute-start.19 = (f32[128,128]{1,0:T(8,128)S(1)}, f32[128,128]{1,0:T(8,128)S(1)}, u32[]{:S(2)}, u32[]{:S(2)}) collective-permute-start(f32[128,128]{1,0:T(8,128)S(1)} %fusion.55), channel_id=1, source_target_pairs={{0,15},{1,0},{2,1},{3,2},{4,3},{5,4},{6,5},{7,6},{8,7},{9,8},{10,9... | collective-permute-start | bytes 196616 | tf_op jit(solution)/shard_map/ppermute | solution.py:25
  151.7 4.8 %collective-permute-start.12 = (f32[128,128]{1,0:T(8,128)S(1)}, f32[128,128]{1,0:T(8,128)S(1)}, u32[]{:S(2)}, u32[]{:S(2)}) collective-permute-start(f32[128,128]{1,0:T(8,128)S(1)} %collective-permute-done.10), channel_id=1, source_target_pairs={{0,15},{1,0},{2,1},{3,2},{4,3},{5,4},{6,5},{7,6},{8,7},{9,8},{10,9... | collective-permute-start | bytes 196616 | tf_op jit(solution)/shard_map/ppermute | solution.py:25
  151.8 7.4 %collective-permute-start.13 = (f32[128,128]{1,0:T(8,128)S(1)}, f32[128,128]{1,0:T(8,128)S(1)}, u32[]{:S(2)}, u32[]{:S(2)}) collective-permute-start(f32[128,128]{1,0:T(8,128)S(1)} %collective-permute-done.11), channel_id=1, source_target_pairs={{0,15},{1,0},{2,1},{3,2},{4,3},{5,4},{6,5},{7,6},{8,7},{9,8},{10,9... | collective-permute-start | bytes 196616 | tf_op jit(solution)/shard_map/ppermute | solution.py:25
  157.3 10.2 %collective-permute-start.25 = (f32[128,128]{1,0:T(8,128)S(1)}, f32[128,128]{1,0:T(8,128)S(1)}, u32[]{:S(2)}, u32[]{:S(2)}) collective-permute-start(f32[128,128]{1,0:T(8,128)S(1)} %add.357), channel_id=1, source_target_pairs={{0,15},{1,0},{2,1},{3,2},{4,3},{5,4},{6,5},{7,6},{8,7},{9,8},{10,9... | collective-permute-start | bytes 196616 | tf_op jit(solution)/shard_map/ppermute | solution.py:25
  159.9 10.1 %collective-permute-start.20 = (f32[128,128]{1,0:T(8,128)S(1)}, f32[128,128]{1,0:T(8,128)S(1)}, u32[]{:S(2)}, u32[]{:S(2)}) collective-permute-start(f32[128,128]{1,0:T(8,128)S(1)} %add.351), channel_id=1, source_target_pairs={{0,15},{1,0},{2,1},{3,2},{4,3},{5,4},{6,5},{7,6},{8,7},{9,8},{10,9... | collective-permute-start | bytes 196616 | tf_op jit(solution)/shard_map/ppermute | solution.py:25
  161.9 4.9 %collective-permute-start.14 = (f32[128,128]{1,0:T(8,128)S(1)}, f32[128,128]{1,0:T(8,128)S(1)}, u32[]{:S(2)}, u32[]{:S(2)}) collective-permute-start(f32[128,128]{1,0:T(8,128)S(1)} %collective-permute-done.12), channel_id=1, source_target_pairs={{0,15},{1,0},{2,1},{3,2},{4,3},{5,4},{6,5},{7,6},{8,7},{9,8},{10,9... | collective-permute-start | bytes 196616 | tf_op jit(solution)/shard_map/ppermute | solution.py:25
  162.4 6.8 %collective-permute-start.15 = (f32[128,128]{1,0:T(8,128)S(1)}, f32[128,128]{1,0:T(8,128)S(1)}, u32[]{:S(2)}, u32[]{:S(2)}) collective-permute-start(f32[128,128]{1,0:T(8,128)S(1)} %collective-permute-done.13), channel_id=1, source_target_pairs={{0,15},{1,0},{2,1},{3,2},{4,3},{5,4},{6,5},{7,6},{8,7},{9,8},{10,9... | collective-permute-start | bytes 196616 | tf_op jit(solution)/shard_map/ppermute | solution.py:25
  167.6 67.7 %collective-permute-start.26 = (f32[128,128]{1,0:T(8,128)S(1)}, f32[128,128]{1,0:T(8,128)S(1)}, u32[]{:S(2)}, u32[]{:S(2)}) collective-permute-start(f32[128,128]{1,0:T(8,128)S(1)} %add.358), channel_id=1, source_target_pairs={{0,15},{1,0},{2,1},{3,2},{4,3},{5,4},{6,5},{7,6},{8,7},{9,8},{10,9... | collective-permute-start | bytes 196616 | tf_op jit(solution)/shard_map/ppermute | solution.py:25
  170.1 67.7 %collective-permute-start.21 = (f32[128,128]{1,0:T(8,128)S(1)}, f32[128,128]{1,0:T(8,128)S(1)}, u32[]{:S(2)}, u32[]{:S(2)}) collective-permute-start(f32[128,128]{1,0:T(8,128)S(1)} %add.352), channel_id=1, source_target_pairs={{0,15},{1,0},{2,1},{3,2},{4,3},{5,4},{6,5},{7,6},{8,7},{9,8},{10,9... | collective-permute-start | bytes 196616 | tf_op jit(solution)/shard_map/ppermute | solution.py:25
  172.9 4.3 %collective-permute-start.16 = (f32[128,128]{1,0:T(8,128)S(1)}, f32[128,128]{1,0:T(8,128)S(1)}, u32[]{:S(2)}, u32[]{:S(2)}) collective-permute-start(f32[128,128]{1,0:T(8,128)S(1)} %collective-permute-done.14), channel_id=1, source_target_pairs={{0,15},{1,0},{2,1},{3,2},{4,3},{5,4},{6,5},{7,6},{8,7},{9,8},{10,9... | collective-permute-start | bytes 196616 | tf_op jit(solution)/shard_map/ppermute | solution.py:25
  173.1 63.9 %collective-permute-start.17 = (f32[128,128]{1,0:T(8,128)S(1)}, f32[128,128]{1,0:T(8,128)S(1)}, u32[]{:S(2)}, u32[]{:S(2)}) collective-permute-start(f32[128,128]{1,0:T(8,128)S(1)} %collective-permute-done.15), channel_id=1, source_target_pairs={{0,15},{1,0},{2,1},{3,2},{4,3},{5,4},{6,5},{7,6},{8,7},{9,8},{10,9... | collective-permute-start | bytes 196616 | tf_op jit(solution)/shard_map/ppermute | solution.py:25
  235.4 4.8 %collective-permute-start.27 = (f32[128,64]{1,0:T(8,128)S(1)}, f32[128,64]{1,0:T(8,128)S(1)}, u32[]{:S(2)}, u32[]{:S(2)}) collective-permute-start(f32[128,64]{1,0:T(8,128)S(1)} %slice_select_fusion), channel_id=1, source_target_pairs={{0,16},{16,0},{1,17},{17,1},{2,18},{18,2},{3,19},{19,3},{4,20},{20... | collective-permute-start | bytes 98312 | tf_op jit(solution)/shard_map/ppermute | solution.py:14
  237.3 0.8 copy-start.4
  238.3 4.3 %collective-permute-start.22 = (f32[128,64]{1,0:T(8,128)S(1)}, f32[128,64]{1,0:T(8,128)S(1)}, u32[]{:S(2)}, u32[]{:S(2)}) collective-permute-start(f32[128,64]{1,0:T(8,128)S(1)} %slice_select_fusion.1), channel_id=1, source_target_pairs={{0,16},{16,0},{1,17},{17,1},{2,18},{18,2},{3,19},{19,3},{4,20},{20... | collective-permute-start | bytes 98312 | tf_op jit(solution)/shard_map/ppermute | solution.py:14
Sparse Core Ops, SparseCore 0:
  26.0 90.5 all-reduce.6
  142.3 92.9 all-reduce.4
where the time goes:
time: 251 us; the launch traced here: 250 us
  waiting for transfers between devices  169 us (67%)
  starting transfers between devices  31.6 us (13%)
  between operations  22.4 us (9%)
  matrix products  18.4 us (7%)
  local copies, waits for them, and re-layouts  5.47 us (2%)
  other arithmetic  3.54 us (1%)
    psum x1, waiting for transfers between devices, spread(): return lax.psum(jnp.where(mine, array, jnp.zeros_like(array)), axis)  88.4 us
    psum x1, waiting for transfers between devices, shards(): total_dk, total_dv = lax.psum((sink_dk, sink_dv), ('inner', 'outer'))  57.4 us
    ppermute x24, starting transfers between devices, shifted(): return lax.ppermute(value, axis, pairs)  27.2 us
    ppermute x24, waiting for transfers between devices, shifted(): return lax.ppermute(value, axis, pairs)  21.4 us
  transfers between devices with their start and end apart: 30, of which 12 were waited for; matrix products, arithmetic and copies ran while one was open for 9% of the time, Pallas kernels for 0%

commit v1 on v0

--- a/solution.py
+++ b/solution.py
@@ -16,7 +16,12 @@
 
 def spread(array, axis, root):
     mine = lax.axis_index(axis) == root
-    return lax.psum(jnp.where(mine, array, jnp.zeros_like(array)), axis)
+
+    def turn_the_record(m):
+        carry = jax.lax.all_gather(m, axis_name=axis).sum(axis=0)
+        return carry
+
+    return turn_the_record(jnp.where(mine, array, jnp.zeros_like(array)))
 
 
 def shifted(value, axis, steps):

time: 251 us -> 218 us (0.87)
  waiting for transfers between devices: 169 us -> 108 us
  starting transfers between devices: 31.6 us -> 51.1 us
  matrix products: 18.4 us -> 22.2 us
  other arithmetic: 3.54 us -> 6.33 us
    psum x1 -> x0, waiting for transfers between devices: 88.4 us -> none  [spread(): return lax.psum(jnp.where(mine, array, jnp.zeros_like(array)), axis)]
    ppermute x24, starting transfers between devices: 27.2 us -> 46.5 us  [shifted(): return lax.ppermute(value, axis, pairs)]
    all_gather x0 -> x2, waiting for transfers between devices: none -> 18.6 us  [turn_the_record(): carry = jax.lax.all_gather(m, axis_name=axis).sum(axis=0)]
    psum x1, waiting for transfers between devices: 57.4 us -> 69.1 us  [shards(): total_dk, total_dv = lax.psum((sink_dk, sink_dv), ('inner', 'outer'))]
    ppermute x24, waiting for transfers between devices: 21.4 us -> 15.3 us  [shifted(): return lax.ppermute(value, axis, pairs)]
    ppermute x4, waiting for transfers between devices: 1.64 us -> 5.35 us  [swapped(): lax.ppermute(array, axis, [(i, i ^ 1 << distance) for i in range(lax.axis...]
    reduce_sum x0 -> x2, other arithmetic: none -> 2.57 us  [turn_the_record(): carry = jax.lax.all_gather(m, axis_name=axis).sum(axis=0)]
    unnamed x20 -> x38, local copies, waits for them, and re-layouts: 4.87 us -> 6.15 us
  transfers between devices with their start and end apart: 30 -> 31, of which waited for: 12 -> 14; matrix products, arithmetic and copies ran while one was open for 9% -> 14% of each run, Pallas kernels for 0% -> 0%
where the time goes in v1:
time: 218 us; the launch traced here: 217 us
  waiting for transfers between devices  108 us (50%)
  starting transfers between devices  51.1 us (23%)
  matrix products  22.2 us (10%)
  between operations  22 us (10%)
  local copies, waits for them, and re-layouts  6.76 us (3%)
  other arithmetic  6.33 us (3%)
    psum x1, waiting for transfers between devices, shards(): total_dk, total_dv = lax.psum((sink_dk, sink_dv), ('inner', 'outer'))  69.1 us
    ppermute x24, starting transfers between devices, shifted(): return lax.ppermute(value, axis, pairs)  46.5 us
    all_gather x2, waiting for transfers between devices, turn_the_record(): carry = jax.lax.all_gather(m, axis_name=axis).sum(axis=0)  18.6 us
    ppermute x24, waiting for transfers between devices, shifted(): return lax.ppermute(value, axis, pairs)  15.3 us
    unnamed x38, local copies, waits for them, and re-layouts  6.15 us
    ppermute x4, waiting for transfers between devices, swapped(): lax.ppermute(array, axis, [(i, i ^ 1 << distance) for i in range(lax.axis...  5.35 us
    dot_general x6, matrix products, backward_step(): step_dv = jnp.einsum('hqk,qhd->kd', weights, grad_blk, precision=precise)  4.51 us
    dot_general x6, matrix products, backward_step(): jnp.einsum('hqk,qhd->kd', dscores, query_blk, precision=precise)  4.44 us
  transfers between devices with their start and end apart: 31, of which 14 were waited for; matrix products, arithmetic and copies ran while one was open for 14% of the time, Pallas kernels for 0%

profile of v1, /device:TPU:8, one launch (start us, length us, event | category | flops | bytes accessed | tf_op | source)
XLA Modules:
  0.0 216.8 jit_solution(17355548724396531470)
XLA Ops:
  7.2 0.9 copy.83
  8.1 1.6 collective-permute-start
  10.4 2.5 %collective-permute-done = f32[128,64]{1,0:T(8,128)S(1)} collective-permute-done((f32[128,64]{1,0:T(8,128)S(1)}, f32[128,64]{1,0:T(8,128)S(1)}, u32[]{:S(2)}, u32[]{:S(2)}) %collective-permute-start) | collective-permute-done | bytes 32800 | tf_op jit(solution)/shard_map/ppermute | solution.py:14
  12.9 0.7 fusion.99
  24.1 1.6 collective-permute-start.6
  25.8 1.6 collective-permute-start.1
  27.5 1.3 collective-permute-done.6
  28.8 1.6 collective-permute-start.7
  30.4 2.4 %collective-permute-start.2 = (f32[128,128]{1,0:T(8,128)S(1)}, f32[128,128]{1,0:T(8,128)S(1)}, u32[]{:S(2)}, u32[]{:S(2)}) collective-permute-start(f32[128,128]{1,0:T(8,128)S(1)} %collective-permute-done.1), channel_id=1, source_target_pairs={{0,1},{1,2},{2,3},{3,4},{4,5},{5,6},{6,7},{7,8},{8,9},{9,10},{10,1... | collective-permute-start | bytes 196616 | tf_op jit(solution)/shard_map/ppermute | solution.py:30
  32.7 0.7 fusion.100
  33.6 1.7 collective-permute-start.8
  35.7 1.3 collective-permute-start.3
  37.4 1.8 collective-permute-done.8
  39.5 4.0 %collective-permute-done.3 = f32[128,128]{1,0:T(8,128)S(1)} collective-permute-done((f32[128,128]{1,0:T(8,128)S(1)}, f32[128,128]{1,0:T(8,128)S(1)}, u32[]{:S(2)}, u32[]{:S(2)}) %collective-permute-start.3) | collective-permute-done | bytes 65568 | tf_op jit(solution)/shard_map/ppermute | solution.py:30
  43.9 3.8 %collective-permute-done.9 = f32[128,128]{1,0:T(8,128)S(1)} collective-permute-done((f32[128,128]{1,0:T(8,128)S(1)}, f32[128,128]{1,0:T(8,128)S(1)}, u32[]{:S(2)}, u32[]{:S(2)}) %collective-permute-start.9) | collective-permute-done | bytes 65568 | tf_op jit(solution)/shard_map/ppermute | solution.py:30
  47.7 4.3 %collective-permute-start.11 = (f32[128,128]{1,0:T(8,128)S(1)}, f32[128,128]{1,0:T(8,128)S(1)}, u32[]{:S(2)}, u32[]{:S(2)}) collective-permute-start(f32[128,128]{1,0:T(8,128)S(1)} %collective-permute-done.9), channel_id=1, source_target_pairs={{0,15},{1,0},{2,1},{3,2},{4,3},{5,4},{6,5},{7,6},{8,7},{9,8},{10,9... | collective-permute-start | bytes 196616 | tf_op jit(solution)/shard_map/ppermute | solution.py:30
  52.0 2.1 collective-permute-start.10
  54.6 1.7 collective-permute-start.13
  56.5 2.5 %collective-permute-start.12 = (f32[128,128]{1,0:T(8,128)S(1)}, f32[128,128]{1,0:T(8,128)S(1)}, u32[]{:S(2)}, u32[]{:S(2)}) collective-permute-start(f32[128,128]{1,0:T(8,128)S(1)} %collective-permute-done.10), channel_id=1, source_target_pairs={{0,15},{1,0},{2,1},{3,2},{4,3},{5,4},{6,5},{7,6},{8,7},{9,8},{10,9... | collective-permute-start | bytes 196616 | tf_op jit(solution)/shard_map/ppermute | solution.py:30
  59.4 2.0 collective-permute-start.15
  61.4 3.4 %collective-permute-start.14 = (f32[128,128]{1,0:T(8,128)S(1)}, f32[128,128]{1,0:T(8,128)S(1)}, u32[]{:S(2)}, u32[]{:S(2)}) collective-permute-start(f32[128,128]{1,0:T(8,128)S(1)} %collective-permute-done.12), channel_id=1, source_target_pairs={{0,15},{1,0},{2,1},{3,2},{4,3},{5,4},{6,5},{7,6},{8,7},{9,8},{10,9... | collective-permute-start | bytes 196616 | tf_op jit(solution)/shard_map/ppermute | solution.py:30
  65.2 2.6 %collective-permute-start.17 = (f32[128,128]{1,0:T(8,128)}, f32[128,128]{1,0:T(8,128)}, u32[]{:S(2)}, u32[]{:S(2)}) collective-permute-start(f32[128,128]{1,0:T(8,128)} %collective-permute-done.15), channel_id=1, source_target_pairs={{0,15},{1,0},{2,1},{3,2},{4,3},{5,4},{6,5},{7,6},{8,7},{9,8},{10,9... | collective-permute-start | bytes 196616 | tf_op jit(solution)/shard_map/ppermute | solution.py:30
  67.8 4.5 %collective-permute-start.16 = (f32[128,128]{1,0:T(8,128)S(1)}, f32[128,128]{1,0:T(8,128)S(1)}, u32[]{:S(2)}, u32[]{:S(2)}) collective-permute-start(f32[128,128]{1,0:T(8,128)S(1)} %collective-permute-done.14), channel_id=1, source_target_pairs={{0,15},{1,0},{2,1},{3,2},{4,3},{5,4},{6,5},{7,6},{8,7},{9,8},{10,9... | collective-permute-start | bytes 196616 | tf_op jit(solution)/shard_map/ppermute | solution.py:30
  72.3 1.3 reduce_sum.125
  74.5 1.1 convolution_bitcast_fusion.11
  75.6 18.6 %all-gather.5.cloned.1.call-done = f32[16,128,128]{2,1,0:T(8,128)} async-done(((f32[1,128,128]{2,1,0:T(8,128)}), f32[16,128,128]{2,1,0:T(8,128)}) %all-gather.5.cloned.1.call-update) | async-done | bytes 1048592 | tf_op jit(solution)/shard_map/all_gather | solution.py:21
  94.2 1.3 reduce_sum.158
  98.6 1.0 fusion.49
  100.1 1.6 collective-permute-start.23
  102.1 1.0 fusion.54
  103.1 2.1 collective-permute-start.18
  106.9 1.2 fusion.41
  108.9 1.1 convolution_bitcast_fusion.6
  110.7 1.2 fusion.39
  117.2 1.2 fusion.56
  118.7 1.2 fusion.55
  120.0 0.9 collective-permute-start.19
  120.9 2.3 %collective-permute-done.24 = f32[128,128]{1,0:T(8,128)S(1)} collective-permute-done((f32[128,128]{1,0:T(8,128)S(1)}, f32[128,128]{1,0:T(8,128)S(1)}, u32[]{:S(2)}, u32[]{:S(2)}) %collective-permute-start.24) | collective-permute-done | bytes 65568 | tf_op jit(solution)/shard_map/ppermute | solution.py:30
  123.6 0.8 collective-permute-done.19
  124.4 2.5 %collective-permute-start.20 = (f32[128,128]{1,0:T(8,128)S(1)}, f32[128,128]{1,0:T(8,128)S(1)}, u32[]{:S(2)}, u32[]{:S(2)}) collective-permute-start(f32[128,128]{1,0:T(8,128)S(1)} %add.347), channel_id=1, source_target_pairs={{0,15},{1,0},{2,1},{3,2},{4,3},{5,4},{6,5},{7,6},{8,7},{9,8},{10,9... | collective-permute-start | bytes 196616 | tf_op jit(solution)/shard_map/ppermute | solution.py:30
  127.7 0.8 collective-permute-start.26
  128.8 0.8 copy.153
  129.7 4.6 %collective-permute-start.21 = (f32[128,128]{1,0:T(8,128)S(1)}, f32[128,128]{1,0:T(8,128)S(1)}, u32[]{:S(2)}, u32[]{:S(2)}) collective-permute-start(f32[128,128]{1,0:T(8,128)S(1)} %add.348), channel_id=1, source_target_pairs={{0,15},{1,0},{2,1},{3,2},{4,3},{5,4},{6,5},{7,6},{8,7},{9,8},{10,9... | collective-permute-start | bytes 196616 | tf_op jit(solution)/shard_map/ppermute | solution.py:30
  134.3 69.1 %all-reduce.3.cloned.1.call-done = (f32[128,128]{1,0:T(8,128)}, f32[128,128]{1,0:T(8,128)}) async-done(((f32[128,128]{1,0:T(8,128)}, f32[128,128]{1,0:T(8,128)}), (f32[128,128]{1,0:T(8,128)}, f32[128,128]{1,0:T(8,128)})) %all-reduce.3.cloned.1.call-update) | async-done | bytes 131088 | tf_op jit(solution)/shard_map/psum | solution.py:168
  203.5 1.5 collective-permute-start.27
  205.1 0.7 collective-permute-start.22
  205.9 2.0 collective-permute-done.27
  208.6 0.9 collective-permute-done.22
  (137 shorter events, 23.3 us)
Async XLA Ops:
  7.2 29.8 %copy-start = (f32[128,4,128]{2,1,0:T(4,128)S(1)}, f32[128,4,128]{2,1,0:T(4,128)}, u32[]{:S(2)}) copy-start(f32[128,4,128]{2,1,0:T(4,128)} %param.15) | copy-start | bytes 786436
  7.2 2.5 %copy-start.14 = (f32[128,64]{0,1:T(8,128)S(1)}, f32[128,64]{0,1:T(8,128)}, u32[]{:S(2)}) copy-start(f32[128,64]{0,1:T(8,128)} %param.17) | copy-start | bytes 98308
  7.2 65.1 %all-gather.3.cloned.1.call-start = ((), (), s32[]{:S(2)}) async-start(), calls=%async_computation | async-start | bytes 1114112 | tf_op jit(solution)/shard_map/all_gather | solution.py:21
  8.1 4.8 %collective-permute-start = (f32[128,64]{1,0:T(8,128)S(1)}, f32[128,64]{1,0:T(8,128)S(1)}, u32[]{:S(2)}, u32[]{:S(2)}) collective-permute-start(f32[128,64]{1,0:T(8,128)S(1)} %copy.83), channel_id=1, source_target_pairs={{0,16},{16,0},{1,17},{17,1},{2,18},{18,2},{3,19},{19,3},{4,20},{20... | collective-permute-start | bytes 98312 | tf_op jit(solution)/shard_map/ppermute | solution.py:14
  9.8 14.2 %collective-permute-start.5 = (f32[128,64]{1,0:T(8,128)S(1)}, f32[128,64]{1,0:T(8,128)S(1)}, u32[]{:S(2)}, u32[]{:S(2)}) collective-permute-start(f32[128,64]{1,0:T(8,128)S(1)} %copy.98), channel_id=1, source_target_pairs={{0,16},{16,0},{1,17},{17,1},{2,18},{18,2},{3,19},{19,3},{4,20},{20... | collective-permute-start | bytes 98312 | tf_op jit(solution)/shard_map/ppermute | solution.py:14
  13.7 0.7 copy-start.15
  13.7 10.2 %copy-start.1 = (f32[128,4,128]{2,1,0:T(4,128)S(1)}, f32[128,4,128]{2,1,0:T(4,128)}, u32[]{:S(2)}) copy-start(f32[128,4,128]{2,1,0:T(4,128)} %param.18) | copy-start | bytes 786436
  13.7 80.5 %all-gather.5.cloned.1.call-start = ((), (), s32[]{:S(2)}) async-start(), calls=%async_computation.1 | async-start | bytes 1114112 | tf_op jit(solution)/shard_map/all_gather | solution.py:21
  24.1 4.7 %collective-permute-start.6 = (f32[128,128]{1,0:T(8,128)S(1)}, f32[128,128]{1,0:T(8,128)S(1)}, u32[]{:S(2)}, u32[]{:S(2)}) collective-permute-start(f32[128,128]{1,0:T(8,128)S(1)} %maximum_select_fusion.2), channel_id=1, source_target_pairs={{0,1},{1,2},{2,3},{3,4},{4,5},{5,6},{6,7},{7,8},{8,9},{9,10},{10,1... | collective-permute-start | bytes 196616 | tf_op jit(solution)/shard_map/ppermute | solution.py:30
  25.8 4.5 %collective-permute-start.1 = (f32[128,128]{1,0:T(8,128)S(1)}, f32[128,128]{1,0:T(8,128)S(1)}, u32[]{:S(2)}, u32[]{:S(2)}) collective-permute-start(f32[128,128]{1,0:T(8,128)S(1)} %maximum_select_fusion), channel_id=1, source_target_pairs={{0,1},{1,2},{2,3},{3,4},{4,5},{5,6},{6,7},{7,8},{8,9},{9,10},{10,1... | collective-permute-start | bytes 196616 | tf_op jit(solution)/shard_map/ppermute | solution.py:30
  28.8 4.8 %collective-permute-start.7 = (f32[128,128]{1,0:T(8,128)S(1)}, f32[128,128]{1,0:T(8,128)S(1)}, u32[]{:S(2)}, u32[]{:S(2)}) collective-permute-start(f32[128,128]{1,0:T(8,128)S(1)} %collective-permute-done.6), channel_id=1, source_target_pairs={{0,1},{1,2},{2,3},{3,4},{4,5},{5,6},{6,7},{7,8},{8,9},{9,10},{10,1... | collective-permute-start | bytes 196616 | tf_op jit(solution)/shard_map/ppermute | solution.py:30
  30.4 5.4 %collective-permute-start.2 = (f32[128,128]{1,0:T(8,128)S(1)}, f32[128,128]{1,0:T(8,128)S(1)}, u32[]{:S(2)}, u32[]{:S(2)}) collective-permute-start(f32[128,128]{1,0:T(8,128)S(1)} %collective-permute-done.1), channel_id=1, source_target_pairs={{0,1},{1,2},{2,3},{3,4},{4,5},{5,6},{6,7},{7,8},{8,9},{9,10},{10,1... | collective-permute-start | bytes 196616 | tf_op jit(solution)/shard_map/ppermute | solution.py:30
  33.5 169.9 %all-reduce.3.cloned.1.call-start = ((), (), s32[]{:S(2)}) async-start(), calls=%async_computation.2 | async-start | bytes 262144 | tf_op jit(solution)/shard_map/psum | solution.py:168
  33.6 5.7 %collective-permute-start.8 = (f32[128,128]{1,0:T(8,128)S(1)}, f32[128,128]{1,0:T(8,128)S(1)}, u32[]{:S(2)}, u32[]{:S(2)}) collective-permute-start(f32[128,128]{1,0:T(8,128)S(1)} %collective-permute-done.7), channel_id=1, source_target_pairs={{0,1},{1,2},{2,3},{3,4},{4,5},{5,6},{6,7},{7,8},{8,9},{9,10},{10,1... | collective-permute-start | bytes 196616 | tf_op jit(solution)/shard_map/ppermute | solution.py:30
  35.7 7.8 %collective-permute-start.3 = (f32[128,128]{1,0:T(8,128)S(1)}, f32[128,128]{1,0:T(8,128)S(1)}, u32[]{:S(2)}, u32[]{:S(2)}) collective-permute-start(f32[128,128]{1,0:T(8,128)S(1)} %collective-permute-done.2), channel_id=1, source_target_pairs={{0,1},{1,2},{2,3},{3,4},{4,5},{5,6},{6,7},{7,8},{8,9},{9,10},{10,1... | collective-permute-start | bytes 196616 | tf_op jit(solution)/shard_map/ppermute | solution.py:30
  39.2 8.5 %collective-permute-start.9 = (f32[128,128]{1,0:T(8,128)S(1)}, f32[128,128]{1,0:T(8,128)S(1)}, u32[]{:S(2)}, u32[]{:S(2)}) collective-permute-start(f32[128,128]{1,0:T(8,128)S(1)} %collective-permute-done.8), channel_id=1, source_target_pairs={{0,1},{1,2},{2,3},{3,4},{4,5},{5,6},{6,7},{7,8},{8,9},{9,10},{10,1... | collective-permute-start | bytes 196616 | tf_op jit(solution)/shard_map/ppermute | solution.py:30
  43.5 8.5 %collective-permute-start.4 = (f32[128,128]{1,0:T(8,128)S(1)}, f32[128,128]{1,0:T(8,128)S(1)}, u32[]{:S(2)}, u32[]{:S(2)}) collective-permute-start(f32[128,128]{1,0:T(8,128)S(1)} %collective-permute-done.3), channel_id=1, source_target_pairs={{0,1},{1,2},{2,3},{3,4},{4,5},{5,6},{6,7},{7,8},{8,9},{9,10},{10,1... | collective-permute-start | bytes 196616 | tf_op jit(solution)/shard_map/ppermute | solution.py:30
  47.7 6.9 %collective-permute-start.11 = (f32[128,128]{1,0:T(8,128)S(1)}, f32[128,128]{1,0:T(8,128)S(1)}, u32[]{:S(2)}, u32[]{:S(2)}) collective-permute-start(f32[128,128]{1,0:T(8,128)S(1)} %collective-permute-done.9), channel_id=1, source_target_pairs={{0,15},{1,0},{2,1},{3,2},{4,3},{5,4},{6,5},{7,6},{8,7},{9,8},{10,9... | collective-permute-start | bytes 196616 | tf_op jit(solution)/shard_map/ppermute | solution.py:30
  52.0 4.5 %collective-permute-start.10 = (f32[128,128]{1,0:T(8,128)S(1)}, f32[128,128]{1,0:T(8,128)S(1)}, u32[]{:S(2)}, u32[]{:S(2)}) collective-permute-start(f32[128,128]{1,0:T(8,128)S(1)} %collective-permute-done.4), channel_id=1, source_target_pairs={{0,15},{1,0},{2,1},{3,2},{4,3},{5,4},{6,5},{7,6},{8,7},{9,8},{10,9... | collective-permute-start | bytes 196616 | tf_op jit(solution)/shard_map/ppermute | solution.py:30
  54.5 4.8 %copy-start.12 = (f32[128,128]{1,0:T(8,128)}, f32[128,128]{1,0:T(8,128)S(1)}, u32[]{:S(2)}) copy-start(f32[128,128]{1,0:T(8,128)S(1)} %collective-permute-done.11) | copy-start | bytes 196612
  54.6 4.8 %collective-permute-start.13 = (f32[128,128]{1,0:T(8,128)S(1)}, f32[128,128]{1,0:T(8,128)S(1)}, u32[]{:S(2)}, u32[]{:S(2)}) collective-permute-start(f32[128,128]{1,0:T(8,128)S(1)} %collective-permute-done.11), channel_id=1, source_target_pairs={{0,15},{1,0},{2,1},{3,2},{4,3},{5,4},{6,5},{7,6},{8,7},{9,8},{10,9... | collective-permute-start | bytes 196616 | tf_op jit(solution)/shard_map/ppermute | solution.py:30
  56.5 4.9 %collective-permute-start.12 = (f32[128,128]{1,0:T(8,128)S(1)}, f32[128,128]{1,0:T(8,128)S(1)}, u32[]{:S(2)}, u32[]{:S(2)}) collective-permute-start(f32[128,128]{1,0:T(8,128)S(1)} %collective-permute-done.10), channel_id=1, source_target_pairs={{0,15},{1,0},{2,1},{3,2},{4,3},{5,4},{6,5},{7,6},{8,7},{9,8},{10,9... | collective-permute-start | bytes 196616 | tf_op jit(solution)/shard_map/ppermute | solution.py:30
  59.4 5.8 %collective-permute-start.15 = (f32[128,128]{1,0:T(8,128)S(1)}, f32[128,128]{1,0:T(8,128)}, u32[]{:S(2)}, u32[]{:S(2)}) collective-permute-start(f32[128,128]{1,0:T(8,128)S(1)} %collective-permute-done.13), channel_id=1, source_target_pairs={{0,15},{1,0},{2,1},{3,2},{4,3},{5,4},{6,5},{7,6},{8,7},{9,8},{10,9... | collective-permute-start | bytes 196616 | tf_op jit(solution)/shard_map/ppermute | solution.py:30
  61.4 43.8 %copy-start.2 = (f32[128,128]{1,0:T(8,128)}, f32[128,128]{1,0:T(8,128)S(1)}, u32[]{:S(2)}) copy-start(f32[128,128]{1,0:T(8,128)S(1)} %collective-permute-done.12) | copy-start | bytes 196612
  61.4 6.4 %collective-permute-start.14 = (f32[128,128]{1,0:T(8,128)S(1)}, f32[128,128]{1,0:T(8,128)S(1)}, u32[]{:S(2)}, u32[]{:S(2)}) collective-permute-start(f32[128,128]{1,0:T(8,128)S(1)} %collective-permute-done.12), channel_id=1, source_target_pairs={{0,15},{1,0},{2,1},{3,2},{4,3},{5,4},{6,5},{7,6},{8,7},{9,8},{10,9... | collective-permute-start | bytes 196616 | tf_op jit(solution)/shard_map/ppermute | solution.py:30
  65.2 44.8 %collective-permute-start.17 = (f32[128,128]{1,0:T(8,128)}, f32[128,128]{1,0:T(8,128)}, u32[]{:S(2)}, u32[]{:S(2)}) collective-permute-start(f32[128,128]{1,0:T(8,128)} %collective-permute-done.15), channel_id=1, source_target_pairs={{0,15},{1,0},{2,1},{3,2},{4,3},{5,4},{6,5},{7,6},{8,7},{9,8},{10,9... | collective-permute-start | bytes 196616 | tf_op jit(solution)/shard_map/ppermute | solution.py:30
  67.8 38.6 %copy-start.4 = (f32[128,128]{1,0:T(8,128)}, f32[128,128]{1,0:T(8,128)S(1)}, u32[]{:S(2)}) copy-start(f32[128,128]{1,0:T(8,128)S(1)} %collective-permute-done.14) | copy-start | bytes 196612
  67.8 40.7 %collective-permute-start.16 = (f32[128,128]{1,0:T(8,128)S(1)}, f32[128,128]{1,0:T(8,128)S(1)}, u32[]{:S(2)}, u32[]{:S(2)}) collective-permute-start(f32[128,128]{1,0:T(8,128)S(1)} %collective-permute-done.14), channel_id=1, source_target_pairs={{0,15},{1,0},{2,1},{3,2},{4,3},{5,4},{6,5},{7,6},{8,7},{9,8},{10,9... | collective-permute-start | bytes 196616 | tf_op jit(solution)/shard_map/ppermute | solution.py:30
  74.5 34.4 %copy-start.6 = (f32[4,128]{1,0:T(4,128)}, f32[4,128]{1,0:T(4,128)S(1)}, u32[]{:S(2)}) copy-start(f32[4,128]{1,0:T(4,128)S(1)} %get-tuple-element.56) | copy-start | bytes 6148
  98.2 8.6 %copy-start.8 = (f32[4,128]{1,0:T(4,128)}, f32[4,128]{1,0:T(4,128)S(1)}, u32[]{:S(2)}) copy-start(f32[4,128]{1,0:T(4,128)S(1)} %div.7) | copy-start | bytes 6148
  100.1 17.1 %collective-permute-start.23 = (f32[128,128]{1,0:T(8,128)}, f32[128,128]{1,0:T(8,128)}, u32[]{:S(2)}, u32[]{:S(2)}) collective-permute-start(f32[128,128]{1,0:T(8,128)} %convolution_bitcast_fusion.11), channel_id=1, source_target_pairs={{0,15},{1,0},{2,1},{3,2},{4,3},{5,4},{6,5},{7,6},{8,7},{9,8},{10,9... | collective-permute-start | bytes 196616 | tf_op jit(solution)/shard_map/ppermute | solution.py:30
  103.1 15.6 %collective-permute-start.18 = (f32[128,128]{1,0:T(8,128)}, f32[128,128]{1,0:T(8,128)}, u32[]{:S(2)}, u32[]{:S(2)}) collective-permute-start(f32[128,128]{1,0:T(8,128)} %fusion.54), channel_id=1, source_target_pairs={{0,15},{1,0},{2,1},{3,2},{4,3},{5,4},{6,5},{7,6},{8,7},{9,8},{10,9... | collective-permute-start | bytes 196616 | tf_op jit(solution)/shard_map/ppermute | solution.py:30
  110.0 0.7 copy-start.9
  112.3 0.7 copy-start.7
  113.0 0.7 copy-start.10
  113.0 0.9 copy-start.13
  114.2 0.8 copy-start.3
  115.1 0.8 copy-start.5
  118.4 4.7 %collective-permute-start.24 = (f32[128,128]{1,0:T(8,128)S(1)}, f32[128,128]{1,0:T(8,128)S(1)}, u32[]{:S(2)}, u32[]{:S(2)}) collective-permute-start(f32[128,128]{1,0:T(8,128)S(1)} %fusion.56), channel_id=1, source_target_pairs={{0,15},{1,0},{2,1},{3,2},{4,3},{5,4},{6,5},{7,6},{8,7},{9,8},{10,9... | collective-permute-start | bytes 196616 | tf_op jit(solution)/shard_map/ppermute | solution.py:30
  120.0 4.4 %collective-permute-start.19 = (f32[128,128]{1,0:T(8,128)S(1)}, f32[128,128]{1,0:T(8,128)S(1)}, u32[]{:S(2)}, u32[]{:S(2)}) collective-permute-start(f32[128,128]{1,0:T(8,128)S(1)} %fusion.55), channel_id=1, source_target_pairs={{0,15},{1,0},{2,1},{3,2},{4,3},{5,4},{6,5},{7,6},{8,7},{9,8},{10,9... | collective-permute-start | bytes 196616 | tf_op jit(solution)/shard_map/ppermute | solution.py:30
  123.2 4.5 %collective-permute-start.25 = (f32[128,128]{1,0:T(8,128)S(1)}, f32[128,128]{1,0:T(8,128)S(1)}, u32[]{:S(2)}, u32[]{:S(2)}) collective-permute-start(f32[128,128]{1,0:T(8,128)S(1)} %add.353), channel_id=1, source_target_pairs={{0,15},{1,0},{2,1},{3,2},{4,3},{5,4},{6,5},{7,6},{8,7},{9,8},{10,9... | collective-permute-start | bytes 196616 | tf_op jit(solution)/shard_map/ppermute | solution.py:30
  124.4 5.3 %collective-permute-start.20 = (f32[128,128]{1,0:T(8,128)S(1)}, f32[128,128]{1,0:T(8,128)S(1)}, u32[]{:S(2)}, u32[]{:S(2)}) collective-permute-start(f32[128,128]{1,0:T(8,128)S(1)} %add.347), channel_id=1, source_target_pairs={{0,15},{1,0},{2,1},{3,2},{4,3},{5,4},{6,5},{7,6},{8,7},{9,8},{10,9... | collective-permute-start | bytes 196616 | tf_op jit(solution)/shard_map/ppermute | solution.py:30
  127.7 75.7 %collective-permute-start.26 = (f32[128,128]{1,0:T(8,128)S(1)}, f32[128,128]{1,0:T(8,128)S(1)}, u32[]{:S(2)}, u32[]{:S(2)}) collective-permute-start(f32[128,128]{1,0:T(8,128)S(1)} %add.354), channel_id=1, source_target_pairs={{0,15},{1,0},{2,1},{3,2},{4,3},{5,4},{6,5},{7,6},{8,7},{9,8},{10,9... | collective-permute-start | bytes 196616 | tf_op jit(solution)/shard_map/ppermute | solution.py:30
  129.7 75.3 %collective-permute-start.21 = (f32[128,128]{1,0:T(8,128)S(1)}, f32[128,128]{1,0:T(8,128)S(1)}, u32[]{:S(2)}, u32[]{:S(2)}) collective-permute-start(f32[128,128]{1,0:T(8,128)S(1)} %add.348), channel_id=1, source_target_pairs={{0,15},{1,0},{2,1},{3,2},{4,3},{5,4},{6,5},{7,6},{8,7},{9,8},{10,9... | collective-permute-start | bytes 196616 | tf_op jit(solution)/shard_map/ppermute | solution.py:30
  203.4 1.6 copy-start.11
  203.5 4.3 %collective-permute-start.27 = (f32[128,64]{1,0:T(8,128)S(1)}, f32[128,64]{1,0:T(8,128)S(1)}, u32[]{:S(2)}, u32[]{:S(2)}) collective-permute-start(f32[128,64]{1,0:T(8,128)S(1)} %slice_select_fusion), channel_id=1, source_target_pairs={{0,16},{16,0},{1,17},{17,1},{2,18},{18,2},{3,19},{19,3},{4,20},{20... | collective-permute-start | bytes 98312 | tf_op jit(solution)/shard_map/ppermute | solution.py:14
  205.1 4.3 %collective-permute-start.22 = (f32[128,64]{1,0:T(8,128)S(1)}, f32[128,64]{1,0:T(8,128)S(1)}, u32[]{:S(2)}, u32[]{:S(2)}) collective-permute-start(f32[128,64]{1,0:T(8,128)S(1)} %slice_select_fusion.1), channel_id=1, source_target_pairs={{0,16},{16,0},{1,17},{17,1},{2,18},{18,2},{3,19},{19,3},{4,20},{20... | collective-permute-start | bytes 98312 | tf_op jit(solution)/shard_map/ppermute | solution.py:14
Sparse Core Ops, SparseCore 0:
  13.8 40.5 all-gather.2
  56.6 37.5 all-gather.4
  112.4 90.8 all-reduce.2
